TPU v7x, 32 devices: a whole 2x2x4 slice. The times are simulated.
32 devices in a mesh: ctx: 8 (over z, y), dp: 4 (over x, core).
Axes of the slice: x: 2, y: 2, z: 4, core: 2. Of those that a mesh axis runs over, the one named last changes fastest.
Arguments:
- grad_out: bfloat16 [4, 3072, 4096], P('dp', 'ctx'), may hold values from -6 to 6
- hidden: bfloat16 [4, 3072, 1792], P('dp', 'ctx'), may hold values from -6 to 6
- down_weight: bfloat16 [1792, 4096], replicated, may hold values from -0.09375 to 0.09375
Outputs:
- grad_hidden: bfloat16 [4, 3072, 1792], P('dp', 'ctx')
- weight_grad: float32 [1792, 4096], P('ctx', 'dp')
- hidden_amax: float32 [4, 1792], P('dp', 'ctx')
- grad_amax: float32 [4, 4096], P('dp', 'ctx')
All inputs are finite; a program needn't handle non-finite values.
Results may differ from a plain program's by a relative error of at most 0.006.
Values may be sent and summed in bfloat16 or wider, within the bound.
A program may use at most 192 MiB of HBM per device.

v0:
```python
import jax
import jax.numpy as jnp
from jax import lax
from jax.sharding import PartitionSpec as P

ceiling = 448.0


def to_grid(values, peaks):
    scaled = values.astype(jnp.float32) * (ceiling / peaks)[None, :]
    magnitude = jnp.abs(scaled)
    spacing = jnp.full_like(magnitude, 2.0 ** (-9))
    for exponent in range(-5, 9):
        spacing = jnp.where(magnitude >= 2.0**exponent, 2.0 ** (exponent - 3), spacing)
    snapped = jnp.floor(magnitude / spacing + 0.5) * spacing
    return jnp.where(scaled < 0, -snapped, snapped).astype(jnp.bfloat16)


def local_peaks(values):
    return jnp.max(jnp.abs(values.astype(jnp.float32)), axis=0)


def on_device(grad_out, hidden, down_weight):
    gdata = grad_out[0]
    hdata = hidden[0]
    ctx_count = lax.axis_size("ctx")
    position = lax.axis_index("ctx")
    ff_rows = hdata.shape[1] // ctx_count
    width_cols = gdata.shape[1] // ctx_count
    seq_total = gdata.shape[0] * ctx_count * lax.axis_size("dp")
    hpeak, gpeak = lax.pmax((local_peaks(hdata), local_peaks(gdata)), "ctx")
    hpeak, gpeak = (jnp.maximum(hpeak, 1.0), jnp.maximum(gpeak, 1.0))
    result = lax.dot_general(
        gdata, down_weight, (((1,), (1,)), ((), ())), preferred_element_type=jnp.float32
    )
    grad_hidden = result.astype(jnp.bfloat16)[None]
    hquant = to_grid(hdata, hpeak)
    gquant = to_grid(gdata, gpeak)
    hscale = hpeak / ceiling
    gscale = gpeak / ceiling
    product = lax.dot_general(
        hquant, gquant, (((0,), (0,)), ((), ())), preferred_element_type=jnp.float32
    )
    partial_value = lax.psum_scatter(
        product * hscale[:, None] * gscale[None, :], "ctx", scatter_dimension=0, tiled=True
    )
    hidden_amax = lax.dynamic_slice_in_dim(hpeak, position * ff_rows, ff_rows, 0)
    summed = lax.psum_scatter(partial_value, "dp", scatter_dimension=1, tiled=True)
    weight_grad = summed / jnp.sqrt(jnp.float32(seq_total))
    grad_amax = lax.dynamic_slice_in_dim(gpeak, position * width_cols, width_cols, 0)
    return (grad_hidden, weight_grad, hidden_amax[None], grad_amax[None])


def solution(mesh):
    placed = (P("dp", "ctx", None), P("dp", "ctx", None), P())
    return jax.shard_map(
        on_device,
        mesh=mesh,
        in_specs=placed,
        out_specs=(P("dp", "ctx", None), P("ctx", "dp"), P("dp", "ctx"), P("dp", "ctx")),
        check_vma=False,
    )
```

profile of v0, /device:TPU:0, one launch (start us, length us, event | category | flops | bytes accessed | tf_op | source)
XLA Modules:
  0.0 590.8 jit_solution(7346190670684098272)
XLA Ops:
  7.2 0.0 copy-start
  7.2 0.0 reduce-scatter.3.cloned.1.call-start
  7.2 2.4 abs_reduce_fusion
  9.6 1.5 fusion.64
  11.1 38.9 %all-reduce = (f32[4096]{0:T(1024)S(1)}, f32[1792]{0:T(1024)S(1)}) all-reduce(f32[4096]{0:T(1024)S(1)} %abs_reduce_fusion, f32[1792]{0:T(1024)S(1)} %fusion.64), channel_id=1, replica_groups=mesh['ctx'=8,'dp'=4] {'ctx'}, use_global_device_ids=true, to_apply=%region_3.0 | all-reduce | flops 5888 | bytes 47104 | tf_op jit(solution)/shard_map/pmax | solution.py:31
  50.0 0.0 copy-done
  50.0 28.1 %multiply_multiply_fusion = f32[1792,4096]{1,0:T(8,128)} fusion(f32[4096]{0:T(1024)S(1)} %get-tuple-element.8, f32[1792]{0:T(1024)S(1)} %get-tuple-element.11, bf16[1,384,4096]{2,1,0:T(8,128)(2,1)S(1)} %copy-done, f32[4096]{0:T(1024)S(1)} %get-tuple-element.7, bf16[1,384,1792]{2,1,0:T(8,128)(2,1)} %param.4, f32[1792]{0:T(1024)S(1)} %get-tuple-element.10), kind=kOutput, calls=%fused_computation | convolution fusion | flops 5740003328 | bytes 33929216 | tf_op jit(solution)/shard_map/dot_general | solution.py:41
  78.1 0.0 reduce-scatter.3.cloned.1.call-update
  78.1 0.0 reduce-scatter.5.cloned.1.call-start
  78.2 460.8 %reduce-scatter.3.cloned.1.call-done = f32[224,4096]{1,0:T(8,128)} async-done(((f32[1792,4096]{1,0:T(8,128)}), f32[224,4096]{1,0:T(8,128)}) %reduce-scatter.3.cloned.1.call-update) | async-done | bytes 3670032 | tf_op jit(solution)/shard_map/reduce_scatter | solution.py:44
  539.0 0.0 reduce-scatter.5.cloned.1.call-update
  539.0 0.7 dynamic_slice.7
  539.7 0.6 dynamic_slice.6
  540.3 10.4 %fusion.66 = bf16[1,384,1792]{2,1,0:T(8,128)(2,1)} fusion(bf16[1792,4096]{1,0:T(8,128)(2,1)} %param.5, bf16[1,384,4096]{2,1,0:T(8,128)(2,1)S(1)} %copy-done), kind=kOutput, calls=%fused_computation.70 | convolution fusion | flops 5637832704 | bytes 19202048 | tf_op jit(solution)/shard_map/dot_general | solution.py:33
  550.7 31.0 %reduce-scatter.5.cloned.1.call-done = f32[224,1024]{1,0:T(8,128)} async-done(((f32[224,4096]{1,0:T(8,128)}), f32[224,1024]{1,0:T(8,128)}) %reduce-scatter.5.cloned.1.call-update) | async-done | bytes 917520 | tf_op jit(solution)/shard_map/reduce_scatter | solution.py:48
  581.8 2.2 broadcast_multiply_fusion
  (2 shorter events, 0.0 us)
Async XLA Ops:
  7.2 42.9 %copy-start = (bf16[1,384,4096]{2,1,0:T(8,128)(2,1)S(1)}, bf16[1,384,4096]{2,1,0:T(8,128)(2,1)}, u32[]{:S(2)}) copy-start(bf16[1,384,4096]{2,1,0:T(8,128)(2,1)} %param.3) | copy-start | bytes 9437188
  7.2 531.8 %reduce-scatter.3.cloned.1.call-start = ((), (), s32[]{:S(2)}) async-start(), calls=%async_computation.2 | async-start | bytes 33030144 | tf_op jit(solution)/shard_map/reduce_scatter | solution.py:44
  78.1 503.6 %reduce-scatter.5.cloned.1.call-start = ((), (), s32[]{:S(2)}) async-start(), calls=%async_computation.3 | async-start | bytes 4587520 | tf_op jit(solution)/shard_map/reduce_scatter | solution.py:48
Sparse Core Ops, SparseCore 0:
  78.2 460.7 reduce-scatter.2
  541.5 40.1 reduce-scatter.4
where the time goes:
time: 591 us
  waiting for transfers between devices  492 us (83%)
  blocking collectives  38.9 us (7%)
  matrix products  38.5 us (7%)
  between operations  14.1 us (2%)
  other arithmetic  6.13 us (1%)
    reduce_scatter x1, waiting for transfers between devices, on_device(): lax.psum_scatter(product * hscale[:, None] * gscale[None, :], 'ctx', scat...  461 us
    pmax x1, blocking collectives, on_device(): hpeak, gpeak = lax.pmax((local_peaks(hdata), local_peaks(gdata)), 'ctx')  38.9 us
    reduce_scatter x1, waiting for transfers between devices, on_device(): lax.psum_scatter(partial_value, 'dp', scatter_dimension=1, tiled=True)  31 us
    dot_general x1, matrix products, on_device(): lax.dot_general(hquant, gquant, (((0,), (0,)), ((), ())), preferred_eleme...  28.1 us
  transfers between devices with their start and end apart: 2, of which 2 were waited for; matrix products, arithmetic and copies ran while one was open for 2% of the time, Pallas kernels for 0%

commit v1 on v0

v1 whole, which is shorter than its diff:
```python
import jax
import jax.numpy as jnp
from jax import lax
from jax.sharding import PartitionSpec as P

ceiling = 448.0
SHARES = (3, 3, 2)


def to_grid(values, peaks):
    scaled = values.astype(jnp.float32) * (ceiling / peaks)
    level = jnp.abs(scaled) * 64.0
    power = jnp.full_like(level, 2.0 ** (-9))
    for step in (8, 4, 2, 1):
        above = level >= 2.0**step
        level = jnp.where(above, level * 2.0**-step, level)
        power = jnp.where(above, power * 2.0**step, power)
    snapped = jnp.floor(level * 8.0 + 0.5) * power
    return jnp.where(scaled < 0, -snapped, snapped).astype(jnp.bfloat16)


def local_peaks(values):
    return jnp.max(jnp.abs(values), axis=0)


def swap(value, axis, bit):
    size = lax.axis_size(axis)
    return lax.ppermute(value, axis, [(i, i ^ (1 << bit)) for i in range(size)])


def bits_of(axis):
    return lax.axis_size(axis).bit_length() - 1


def on_device(grad_out, hidden, down_weight):
    gdata = grad_out[0]
    hdata = hidden[0]
    ctx_count, dp_count = lax.axis_size("ctx"), lax.axis_size("dp")
    ctx_pos, dp_pos = lax.axis_index("ctx"), lax.axis_index("dp")
    ctx_bits, dp_bits = bits_of("ctx"), bits_of("dp")
    tokens, ff = hdata.shape
    width = gdata.shape[1]
    ff_rows, width_cols = ff // ctx_count, width // ctx_count
    outer = dp_count // 2
    unit = width // dp_count // sum(SHARES)
    edges = [unit * sum(SHARES[:c]) for c in range(len(SHARES) + 1)]
    seq_total = tokens * ctx_count * dp_count
    core = dp_pos % 2

    halves = gdata.reshape(tokens, outer, 2, width // dp_count)

    def half(values, which):
        return lax.dynamic_index_in_dim(values, which, values.ndim - 2, keepdims=False)

    gmine = half(halves, core)
    gother = swap(half(halves, 1 - core), "dp", 0)
    hother = swap(hdata, "dp", 0)

    peaks = jnp.concatenate([local_peaks(hdata), local_peaks(gdata)])
    for bit in range(ctx_bits):
        peaks = jnp.maximum(peaks, swap(peaks, "ctx", bit))
    peaks_other = swap(peaks, "dp", 0)
    peaks = jnp.maximum(peaks.astype(jnp.float32), 1.0)
    peaks_other = jnp.maximum(peaks_other.astype(jnp.float32), 1.0)
    hpeak, gpeak = peaks[:ff], peaks[ff:]

    result = lax.dot_general(
        gdata, down_weight, (((1,), (1,)), ((), ())), preferred_element_type=jnp.float32
    )
    grad_hidden = result.astype(jnp.bfloat16)[None]

    sides = []
    for h, g, pk in ((hdata, gmine, peaks), (hother, gother, peaks_other)):
        hp = pk[:ff]
        gp = half(pk[ff:].reshape(outer, 2, width // dp_count), core)
        hq = to_grid(h, hp[None, :])
        gq = to_grid(g, gp[None])
        near = [lax.dynamic_index_in_dim(gq, step ^ (dp_pos // 2), 1, keepdims=False) for step in range(outer)]
        scales = [
            lax.dynamic_index_in_dim(gp / ceiling, step ^ (dp_pos // 2), 0, keepdims=False)
            for step in range(outer)
        ]
        hq, near = lax.optimization_barrier((hq, near))
        sides.append((hq, near, hp / ceiling, scales))

    dp_list = [("dp", bit) for bit in range(1, dp_bits)]
    ctx_list = [("ctx", bit) for bit in range(ctx_bits)]
    orders = [
        dp_list + ctx_list,
        ctx_list[:2] + dp_list + ctx_list[2:],
        ctx_list[1:2] + dp_list + ctx_list[:1] + ctx_list[2:],
    ]

    def block_value(c, step):
        total = None
        cols = slice(edges[c], edges[c + 1])
        for hq, near, hs, scales in sides:
            term = lax.dot_general(
                hq, near[step][:, cols], (((0,), (0,)), ((), ())), preferred_element_type=jnp.float32
            )
            term = term * hs[:, None] * scales[step][None, cols]
            total = term if total is None else total + term
        return total.reshape(ctx_count, ff_rows, -1)

    def split(value, bit, kept):
        low = 1 << (len(kept) - 1 - kept.index(bit))
        shape = value.shape
        view = value.reshape((shape[0] // (2 * low), 2, low) + shape[1:])
        own = ctx_pos // (1 << bit) % 2
        target = (shape[0] // 2,) + shape[1:]
        keep = lax.dynamic_index_in_dim(view, own, 1, keepdims=False).reshape(target)
        send = lax.dynamic_index_in_dim(view, 1 - own, 1, keepdims=False).reshape(target)
        return keep, send

    state = []
    for c in range(len(SHARES)):
        blocks = {step: block_value(c, step) for step in reversed(range(outer))}
        state.append((blocks, list(range(ctx_bits - 1, -1, -1))))
    for stage in range(len(orders[0])):
        for c in range(len(SHARES)):
            blocks, kept = state[c]
            axis, bit = orders[c][stage]
            if axis == "dp":
                far = 1 << (bit - 1)
                blocks = {
                    step: blocks[step]
                    + swap(blocks[step ^ far].astype(jnp.bfloat16), axis, bit).astype(jnp.float32)
                    for step in blocks
                    if not step & far
                }
            else:
                pairs = {step: split(blocks[step], bit, kept) for step in blocks}
                blocks = {
                    step: keep + swap(send.astype(jnp.bfloat16), axis, bit).astype(jnp.float32)
                    for step, (keep, send) in pairs.items()
                }
                kept = [other for other in kept if other != bit]
            state[c] = (blocks, kept)
    weight_grad = jnp.concatenate(
        [blocks[0].reshape(ff_rows, -1) for blocks, _ in state], axis=1
    ) / jnp.sqrt(jnp.float32(seq_total))

    hidden_amax = lax.dynamic_slice_in_dim(hpeak, ctx_pos * ff_rows, ff_rows, 0)
    grad_amax = lax.dynamic_slice_in_dim(gpeak, ctx_pos * width_cols, width_cols, 0)
    return (grad_hidden, weight_grad, hidden_amax[None], grad_amax[None])


def solution(mesh):
    placed = (P("dp", "ctx", None), P("dp", "ctx", None), P())
    return jax.shard_map(
        on_device,
        mesh=mesh,
        in_specs=placed,
        out_specs=(P("dp", "ctx", None), P("ctx", "dp"), P("dp", "ctx"), P("dp", "ctx")),
        check_vma=False,
    )
```

time: 591 us -> 148 us (0.25)
  waiting for transfers between devices: 492 us -> 61.6 us
  blocking collectives: 38.9 us -> 0 us
  starting transfers between devices: 0.08 us -> 20.5 us
  other arithmetic: 6.13 us -> 23.9 us
  local copies, waits for them, and re-layouts: 1.29 us -> 16.4 us
  matrix products: 38.5 us -> 23.6 us
  between operations: 14.1 us -> 1.13 us
    reduce_scatter x2 -> x0, waiting for transfers between devices: 492 us -> none  [the longest x1 461 us: on_device(): lax.psum_scatter(product * hscale[:, None] * gscale[None, :], 'ctx', scat...]
    ppermute x0 -> x21, waiting for transfers between devices: none -> 61.6 us  [swap(): return lax.ppermute(value, axis, [(i, i ^ 1 << bit) for i in range(size)])]
    pmax x1 -> x0, blocking collectives: 38.9 us -> none  [on_device(): hpeak, gpeak = lax.pmax((local_peaks(hdata), local_peaks(gdata)), 'ctx')]
    ppermute x0 -> x21, starting transfers between devices: none -> 20.5 us  [swap(): return lax.ppermute(value, axis, [(i, i ^ 1 << bit) for i in range(size)])]
    convert_element_type x0 -> x6, other arithmetic: none -> 17.8 us  [the longest x4 17.6 us: to_grid(): return jnp.where(scaled < 0, -snapped, snapped).astype(jnp.bfloat16)]
    dot_general x1 -> x12, matrix products: 28.1 us -> 13.2 us  [block_value(): lax.dot_general(hq, near[step][:, cols], (((0,), (0,)), ((), ())), prefer...]
    dynamic_slice x2 -> x12, local copies, waits for them, and re-layouts: 1.29 us -> 10.1 us  [the longest x6 8.62 us: on_device(): lax.dynamic_index_in_dim(gq, step ^ dp_pos // 2, 1, keepdims=False)]
  transfers between devices with their start and end apart: 2 -> 21, of which waited for: 2 -> 8; matrix products, arithmetic and copies ran while one was open for 2% -> 30% of each run, Pallas kernels for 0% -> 0%
where the time goes in v1:
time: 148 us; the launch traced here: 147 us
  waiting for transfers between devices  61.6 us (42%)
  other arithmetic  23.9 us (16%)
  matrix products  23.6 us (16%)
  starting transfers between devices  20.5 us (14%)
  local copies, waits for them, and re-layouts  16.4 us (11%)
    ppermute x21, waiting for transfers between devices, swap(): return lax.ppermute(value, axis, [(i, i ^ 1 << bit) for i in range(size)])  61.6 us
    ppermute x21, starting transfers between devices, swap(): return lax.ppermute(value, axis, [(i, i ^ 1 << bit) for i in range(size)])  20.5 us
    convert_element_type x4, other arithmetic, to_grid(): return jnp.where(scaled < 0, -snapped, snapped).astype(jnp.bfloat16)  17.6 us
    dot_general x12, matrix products, block_value(): lax.dot_general(hq, near[step][:, cols], (((0,), (0,)), ((), ())), prefer...  13.2 us
    dot_general x1, matrix products, on_device(): lax.dot_general(gdata, down_weight, (((1,), (1,)), ((), ())), preferred_e...  10.4 us
    dynamic_slice x6, local copies, waits for them, and re-layouts, on_device(): lax.dynamic_index_in_dim(gq, step ^ dp_pos // 2, 1, keepdims=False)  8.62 us
    reduce_max x2, other arithmetic, local_peaks(): return jnp.max(jnp.abs(values), axis=0)  3.89 us
  transfers between devices with their start and end apart: 21, of which 8 were waited for; matrix products, arithmetic and copies ran while one was open for 30% of the time, Pallas kernels for 0%

profile of v1, /device:TPU:0, one launch (start us, length us, event | category | flops | bytes accessed | tf_op | source)
XLA Modules:
  0.0 147.2 jit_solution(15634401922351091766)
XLA Ops:
  0.6 2.4 %fusion.14 = bf16[4096]{0:T(1024)(128)(2,1)S(1)} fusion(bf16[1,384,4096]{2,1,0:T(8,128)(2,1)} %param.3), kind=kLoop, calls=%fused_computation.52 | loop fusion | flops 3141632 | bytes 3153920 | tf_op jit(solution)/shard_map/reduce_max | solution.py:23
  3.0 1.5 %abs_reduce_fusion = bf16[1792]{0:T(1024)(128)(2,1)S(1)} fusion(bf16[1,384,1792]{2,1,0:T(8,128)(2,1)} %param.4), kind=kLoop, calls=%fused_computation.112 | loop fusion | flops 1374464 | bytes 1379840 | tf_op jit(solution)/shard_map/reduce_max | solution.py:23
  4.5 3.1 %collective-permute-start = (bf16[5888]{0:T(1024)(128)(2,1)S(1)}, bf16[5888]{0:T(1024)(128)(2,1)S(1)}, u32[]{:S(2)}, u32[]{:S(2)}) collective-permute-start(bf16[5888]{0:T(1024)(128)(2,1)S(1)} %pad_maximum_fusion), channel_id=1, source_target_pairs={{0,4},{4,0},{8,12},{12,8},{16,20},{20,16},{24,28},{28,24},{1,5},{5... | collective-permute-start | bytes 35336 | tf_op jit(solution)/shard_map/ppermute | solution.py:28
  7.6 2.8 %copy.12 = bf16[1,384,4096]{1,2,0:T(8,128)(2,1)} copy(bf16[1,384,4096]{2,1,0:T(8,128)(2,1)S(1)} %copy-done) | data formatting | bytes 6291456 | tf_op args[0]
  10.4 1.6 %collective-permute-start.1 = (bf16[5888]{0:T(1024)(128)(2,1)S(1)}, bf16[5888]{0:T(1024)(128)(2,1)S(1)}, u32[]{:S(2)}, u32[]{:S(2)}) collective-permute-start(bf16[5888]{0:T(1024)(128)(2,1)S(1)} %fusion.82), channel_id=1, source_target_pairs={{0,8},{4,12},{8,0},{12,4},{16,24},{20,28},{24,16},{28,20},{1,9},{5... | collective-permute-start | bytes 35336 | tf_op jit(solution)/shard_map/ppermute | solution.py:28
  12.1 2.7 %dynamic-slice_bitcast_fusion = bf16[384,2,1024]{0,2,1:T(8,128)(2,1)} fusion(bf16[384,2,2,1024]{0,3,2,1:T(8,128)(2,1)} %bitcast.137, s32[]{:T(128)S(6)} %select_n.278), kind=kLoop, calls=%fused_computation.105 | loop fusion | bytes 3145732 | tf_op jit(solution)/shard_map/jit(dynamic_index_in_dim)/squeeze | solution.py:53
  14.8 0.5 collective-permute-start.3
  15.3 2.7 %collective-permute-start.2 = (bf16[5888]{0:T(1024)(128)(2,1)S(1)}, bf16[5888]{0:T(1024)(128)(2,1)S(1)}, u32[]{:S(2)}, u32[]{:S(2)}) collective-permute-start(bf16[5888]{0:T(1024)(128)(2,1)S(1)} %max.16), channel_id=1, source_target_pairs={{0,16},{4,20},{8,24},{12,28},{16,0},{20,4},{24,8},{28,12},{1,17},{... | collective-permute-start | bytes 35336 | tf_op jit(solution)/shard_map/ppermute | solution.py:28
  18.0 10.4 %fusion.52 = bf16[1,384,1792]{2,1,0:T(8,128)(2,1)} fusion(bf16[1792,4096]{1,0:T(8,128)(2,1)} %param.5, bf16[1,384,4096]{2,1,0:T(8,128)(2,1)S(1)} %copy-done), kind=kOutput, calls=%fused_computation.104 | convolution fusion | flops 5637832704 | bytes 19202048 | tf_op jit(solution)/shard_map/dot_general | solution.py:67
  28.5 3.9 %fusion.51 = bf16[384,1792]{1,0:T(8,128)(2,1)S(1)} fusion(f32[1792]{0:T(1024)S(1)} %get-tuple-element.31, bf16[1,384,1792]{2,1,0:T(8,128)(2,1)} %param.4), kind=kLoop, calls=%fused_computation.103 | loop fusion | flops 21331968 | bytes 2759680 | tf_op jit(solution)/shard_map/convert_element_type | solution.py:19
  32.4 0.7 dynamic_slice.173
  33.0 0.6 dynamic_slice.172
  33.7 4.4 %fusion.17 = bf16[384,2,1024]{0,2,1:T(8,128)(2,1)S(1)} fusion(f32[2,1024]{1,0:T(2,128)S(1)} %bitcast.174, bf16[384,2,2,1024]{0,3,2,1:T(8,128)(2,1)} %bitcast.138, s32[]{:T(128)S(6)} %select_n.256), kind=kLoop, calls=%fused_computation.56 | loop fusion | flops 24379392 | bytes 3153924 | tf_op jit(solution)/shard_map/convert_element_type | solution.py:19
  38.2 1.0 constant_dynamic-slice_fusion.9
  39.3 0.3 copy.13
  39.6 1.4 copy.14
  41.1 4.7 %fusion.49 = bf16[384,1792]{1,0:T(8,128)(2,1)} fusion(bf16[384,1792]{1,0:T(8,128)(2,1)} %collective-permute-done.3, f32[1792]{0:T(1024)S(1)} %get-tuple-element.34), kind=kLoop, calls=%fused_computation.100 | loop fusion | flops 21331968 | bytes 2759680 | tf_op jit(solution)/shard_map/convert_element_type | solution.py:19
  45.9 4.6 %fusion.16 = bf16[384,2,1024]{0,2,1:T(8,128)(2,1)S(1)} fusion(bf16[384,2,1024]{0,2,1:T(8,128)(2,1)} %collective-permute-done.5, f32[2,1024]{1,0:T(2,128)S(1)} %bitcast.173), kind=kLoop, calls=%fused_computation.55 | loop fusion | flops 24379392 | bytes 3153920 | tf_op jit(solution)/shard_map/convert_element_type | solution.py:19
  50.5 1.3 constant_dynamic-slice_fusion.5
  51.8 2.3 %copy.18 = bf16[384,1,1024]{2,0,1:T(8,128)(2,1)} copy(bf16[384,1,1024]{0,2,1:T(8,128)(2,1)} %get-tuple-element.28) | data formatting | bytes 1572864 | tf_op jit(solution)/shard_map/jit(dynamic_index_in_dim)/dynamic_slice | solution.py:78
  54.1 2.3 %copy.17 = bf16[384,1,1024]{2,0,1:T(8,128)(2,1)} copy(bf16[384,1,1024]{0,2,1:T(8,128)(2,1)} %get-tuple-element.29) | data formatting | bytes 1572864 | tf_op jit(solution)/shard_map/jit(dynamic_index_in_dim)/dynamic_slice | solution.py:78
  56.3 2.4 %fusion.23 = f32[1792,384]{1,0:T(8,128)S(1)} fusion(bf16[384,1792]{1,0:T(8,128)(2,1)} %fusion.49, f32[384]{0:T(512)S(1)} %get-tuple-element.18, f32[1792]{0:T(1024)S(1)} %get-tuple-element.33, bf16[384,1024]{1,0:T(8,128)(2,1)} %bitcast.168), kind=kOutput, calls=%fused_computation.70 | convolution fusion | flops 529858560 | bytes 4432384 | tf_op jit(solution)/shard_map/dot_general | solution.py:98
  58.8 1.2 fusion.33
  60.0 1.6 %collective-permute-start.6 = (bf16[8,224,384]{2,1,0:T(8,128)(2,1)S(1)}, bf16[8,224,384]{2,1,0:T(8,128)(2,1)S(1)}, u32[]{:S(2)}, u32[]{:S(2)}) collective-permute-start(bf16[8,224,384]{2,1,0:T(8,128)(2,1)S(1)} %bitcast.164), channel_id=1, source_target_pairs={{0,2},{1,3},{2,0},{3,1},{4,6},{5,7},{6,4},{7,5},{8,10},{9,11},{10,... | collective-permute-start | bytes 4128776 | tf_op jit(solution)/shard_map/ppermute | solution.py:28
  61.6 1.1 fusion.20
  62.6 1.1 fusion.26
  63.7 1.1 fusion.25
  64.8 0.1 fusion.58
  64.9 1.0 collective-permute-start.10
  65.9 1.1 fusion.29
  67.0 1.1 fusion.28
  68.2 1.2 collective-permute-start.12
  69.4 0.7 fusion.34
  70.1 0.7 fusion.39
  70.9 0.5 collective-permute-start.17
  71.5 0.7 fusion.36
  72.2 0.7 fusion.38
  73.0 1.6 %collective-permute-start.16 = (bf16[4,224,256]{2,1,0:T(8,128)(2,1)S(1)}, bf16[4,224,256]{2,1,0:T(8,128)(2,1)S(1)}, u32[]{:S(2)}, u32[]{:S(2)}) collective-permute-start(bf16[4,224,256]{2,1,0:T(8,128)(2,1)S(1)} %bitcast.171), channel_id=1, source_target_pairs={{0,8},{4,12},{8,0},{12,4},{16,24},{20,28},{24,16},{28,20},{1,9},{5... | collective-permute-start | bytes 1376264 | tf_op jit(solution)/shard_map/ppermute | solution.py:28
  74.6 1.4 fusion.19
  76.0 8.3 %collective-permute-done.17 = bf16[4,224,256]{2,1,0:T(8,128)(2,1)S(1)} collective-permute-done((bf16[4,224,256]{2,1,0:T(8,128)(2,1)S(1)}, bf16[4,224,256]{2,1,0:T(8,128)(2,1)S(1)}, u32[]{:S(2)}, u32[]{:S(2)}) %collective-permute-start.17) | collective-permute-done | bytes 458784 | tf_op jit(solution)/shard_map/ppermute | solution.py:28
  84.3 0.1 fusion.55
  84.5 0.6 collective-permute-start.18
  85.1 0.1 bitcast_add_fusion.1
  85.2 0.5 collective-permute-start.11
  85.8 11.5 %collective-permute-done.12 = bf16[4,224,384]{2,1,0:T(8,128)(2,1)S(1)} collective-permute-done((bf16[4,224,384]{2,1,0:T(8,128)(2,1)S(1)}, bf16[4,224,384]{2,1,0:T(8,128)(2,1)S(1)}, u32[]{:S(2)}, u32[]{:S(2)}) %collective-permute-start.12) | collective-permute-done | bytes 688160 | tf_op jit(solution)/shard_map/ppermute | solution.py:28
  97.3 0.1 bitcast_add_fusion
  97.5 0.5 collective-permute-start.13
  98.0 4.5 %collective-permute-done.18 = bf16[4,224,256]{2,1,0:T(8,128)(2,1)S(1)} collective-permute-done((bf16[4,224,256]{2,1,0:T(8,128)(2,1)S(1)}, bf16[4,224,256]{2,1,0:T(8,128)(2,1)S(1)}, u32[]{:S(2)}, u32[]{:S(2)}) %collective-permute-start.18) | collective-permute-done | bytes 458784 | tf_op jit(solution)/shard_map/ppermute | solution.py:28
  102.5 0.2 fusion.56
  102.7 1.0 collective-permute-start.19
  103.7 0.2 convert_add_fusion
  104.0 1.2 collective-permute-start.7
  105.2 6.0 %collective-permute-done.19 = bf16[2,224,256]{2,1,0:T(8,128)(2,1)S(1)} collective-permute-done((bf16[2,224,256]{2,1,0:T(8,128)(2,1)S(1)}, bf16[2,224,256]{2,1,0:T(8,128)(2,1)S(1)}, u32[]{:S(2)}, u32[]{:S(2)}) %collective-permute-start.19) | collective-permute-done | bytes 229408 | tf_op jit(solution)/shard_map/ppermute | solution.py:28
  111.3 0.4 collective-permute-start.20
  111.8 1.6 %collective-permute-start.14 = (bf16[2,224,384]{2,1,0:T(8,128)(2,1)S(1)}, bf16[2,224,384]{2,1,0:T(8,128)(2,1)S(1)}, u32[]{:S(2)}, u32[]{:S(2)}) collective-permute-start(bf16[2,224,384]{2,1,0:T(8,128)(2,1)S(1)} %fusion.60), channel_id=1, source_target_pairs={{0,2},{1,3},{2,0},{3,1},{4,6},{5,7},{6,4},{7,5},{8,10},{9,11},{10,... | collective-permute-start | bytes 1032200 | tf_op jit(solution)/shard_map/ppermute | solution.py:28
  113.4 4.8 %collective-permute-done.20 = bf16[1,224,256]{2,1,0:T(8,128)(2,1)S(1)} collective-permute-done((bf16[1,224,256]{2,1,0:T(8,128)(2,1)S(1)}, bf16[1,224,256]{2,1,0:T(8,128)(2,1)S(1)}, u32[]{:S(2)}, u32[]{:S(2)}) %collective-permute-start.20) | collective-permute-done | bytes 114720 | tf_op jit(solution)/shard_map/ppermute | solution.py:28
  118.2 6.4 %collective-permute-done.7 = bf16[4,224,384]{2,1,0:T(8,128)(2,1)S(1)} collective-permute-done((bf16[4,224,384]{2,1,0:T(8,128)(2,1)S(1)}, bf16[4,224,384]{2,1,0:T(8,128)(2,1)S(1)}, u32[]{:S(2)}, u32[]{:S(2)}) %collective-permute-start.7) | collective-permute-done | bytes 688160 | tf_op jit(solution)/shard_map/ppermute | solution.py:28
  124.6 0.1 bitcast_add_fusion.2
  124.8 0.5 collective-permute-start.8
  125.4 0.1 fusion.61
  125.5 0.4 collective-permute-start.15
  125.9 11.4 %collective-permute-done.8 = bf16[2,224,384]{2,1,0:T(8,128)(2,1)S(1)} collective-permute-done((bf16[2,224,384]{2,1,0:T(8,128)(2,1)S(1)}, bf16[2,224,384]{2,1,0:T(8,128)(2,1)S(1)}, u32[]{:S(2)}, u32[]{:S(2)}) %collective-permute-start.8) | collective-permute-done | bytes 344096 | tf_op jit(solution)/shard_map/ppermute | solution.py:28
  137.6 8.5 %collective-permute-done.9 = bf16[1,224,384]{2,1,0:T(8,128)(2,1)S(1)} collective-permute-done((bf16[1,224,384]{2,1,0:T(8,128)(2,1)S(1)}, bf16[1,224,384]{2,1,0:T(8,128)(2,1)S(1)}, u32[]{:S(2)}, u32[]{:S(2)}) %collective-permute-start.9) | collective-permute-done | bytes 172064 | tf_op jit(solution)/shard_map/ppermute | solution.py:28
  146.1 1.0 maximum_multiply_fusion
  (67 shorter events, 1.4 us)
Async XLA Ops:
  0.6 7.0 %copy-start = (bf16[1,384,4096]{2,1,0:T(8,128)(2,1)S(1)}, bf16[1,384,4096]{2,1,0:T(8,128)(2,1)}, u32[]{:S(2)}) copy-start(bf16[1,384,4096]{2,1,0:T(8,128)(2,1)} %param.3) | copy-start | bytes 9437188
  4.5 5.9 %collective-permute-start = (bf16[5888]{0:T(1024)(128)(2,1)S(1)}, bf16[5888]{0:T(1024)(128)(2,1)S(1)}, u32[]{:S(2)}, u32[]{:S(2)}) collective-permute-start(bf16[5888]{0:T(1024)(128)(2,1)S(1)} %pad_maximum_fusion), channel_id=1, source_target_pairs={{0,4},{4,0},{8,12},{12,8},{16,20},{20,16},{24,28},{28,24},{1,5},{5... | collective-permute-start | bytes 35336 | tf_op jit(solution)/shard_map/ppermute | solution.py:28
  10.4 4.9 %collective-permute-start.1 = (bf16[5888]{0:T(1024)(128)(2,1)S(1)}, bf16[5888]{0:T(1024)(128)(2,1)S(1)}, u32[]{:S(2)}, u32[]{:S(2)}) collective-permute-start(bf16[5888]{0:T(1024)(128)(2,1)S(1)} %fusion.82), channel_id=1, source_target_pairs={{0,8},{4,12},{8,0},{12,4},{16,24},{20,28},{24,16},{28,20},{1,9},{5... | collective-permute-start | bytes 35336 | tf_op jit(solution)/shard_map/ppermute | solution.py:28
  14.8 31.1 %collective-permute-start.5 = (bf16[384,2,1024]{0,2,1:T(8,128)(2,1)}, bf16[384,2,1024]{0,2,1:T(8,128)(2,1)}, u32[]{:S(2)}, u32[]{:S(2)}) collective-permute-start(bf16[384,2,1024]{0,2,1:T(8,128)(2,1)} %dynamic-slice_bitcast_fusion), channel_id=1, source_target_pairs={{0,1},{1,0},{2,3},{3,2},{4,5},{5,4},{6,7},{7,6},{8,9},{9,8},{10,11... | collective-permute-start | bytes 4718600 | tf_op jit(solution)/shard_map/ppermute | solution.py:28
  14.8 26.3 %collective-permute-start.3 = (bf16[384,1792]{1,0:T(8,128)(2,1)}, bf16[384,1792]{1,0:T(8,128)(2,1)}, u32[]{:S(2)}, u32[]{:S(2)}) collective-permute-start(bf16[384,1792]{1,0:T(8,128)(2,1)} %bitcast.2), channel_id=1, source_target_pairs={{0,1},{1,0},{2,3},{3,2},{4,5},{5,4},{6,7},{7,6},{8,9},{9,8},{10,11... | collective-permute-start | bytes 4128776 | tf_op jit(solution)/shard_map/ppermute | solution.py:28
  15.3 13.1 %collective-permute-start.2 = (bf16[5888]{0:T(1024)(128)(2,1)S(1)}, bf16[5888]{0:T(1024)(128)(2,1)S(1)}, u32[]{:S(2)}, u32[]{:S(2)}) collective-permute-start(bf16[5888]{0:T(1024)(128)(2,1)S(1)} %max.16), channel_id=1, source_target_pairs={{0,16},{4,20},{8,24},{12,28},{16,0},{20,4},{24,8},{28,12},{1,17},{... | collective-permute-start | bytes 35336 | tf_op jit(solution)/shard_map/ppermute | solution.py:28
  28.4 5.3 %collective-permute-start.4 = (bf16[5888]{0:T(1024)(128)(2,1)S(1)}, bf16[5888]{0:T(1024)(128)(2,1)S(1)}, u32[]{:S(2)}, u32[]{:S(2)}) collective-permute-start(bf16[5888]{0:T(1024)(128)(2,1)S(1)} %get-tuple-element.25), channel_id=1, source_target_pairs={{0,1},{1,0},{2,3},{3,2},{4,5},{5,4},{6,7},{7,6},{8,9},{9,8},{10,11... | collective-permute-start | bytes 35336 | tf_op jit(solution)/shard_map/ppermute | solution.py:28
  58.8 2.8 %copy-start.1 = (bf16[384,1792]{1,0:T(8,128)(2,1)S(1)}, bf16[384,1792]{1,0:T(8,128)(2,1)}, u32[]{:S(2)}) copy-start(bf16[384,1792]{1,0:T(8,128)(2,1)} %fusion.49) | copy-start | bytes 4128772
  58.8 2.8 %copy-start.2 = (bf16[384,1,1024]{2,0,1:T(8,128)(2,1)S(1)}, bf16[384,1,1024]{2,0,1:T(8,128)(2,1)}, u32[]{:S(2)}) copy-start(bf16[384,1,1024]{2,0,1:T(8,128)(2,1)} %copy.17) | copy-start | bytes 2359300
  60.0 43.7 %collective-permute-start.6 = (bf16[8,224,384]{2,1,0:T(8,128)(2,1)S(1)}, bf16[8,224,384]{2,1,0:T(8,128)(2,1)S(1)}, u32[]{:S(2)}, u32[]{:S(2)}) collective-permute-start(bf16[8,224,384]{2,1,0:T(8,128)(2,1)S(1)} %bitcast.164), channel_id=1, source_target_pairs={{0,2},{1,3},{2,0},{3,1},{4,6},{5,7},{6,4},{7,5},{8,10},{9,11},{10,... | collective-permute-start | bytes 4128776 | tf_op jit(solution)/shard_map/ppermute | solution.py:28
  63.7 2.2 %copy-start.3 = (bf16[384,1,1024]{2,0,1:T(8,128)(2,1)S(1)}, bf16[384,1,1024]{2,0,1:T(8,128)(2,1)}, u32[]{:S(2)}) copy-start(bf16[384,1,1024]{2,0,1:T(8,128)(2,1)} %copy.18) | copy-start | bytes 2359300
  64.9 20.1 %collective-permute-start.10 = (bf16[4,224,384]{2,1,0:T(8,128)(2,1)S(1)}, bf16[4,224,384]{2,1,0:T(8,128)(2,1)S(1)}, u32[]{:S(2)}, u32[]{:S(2)}) collective-permute-start(bf16[4,224,384]{2,1,0:T(8,128)(2,1)S(1)} %fusion.58), channel_id=1, source_target_pairs={{0,4},{4,0},{8,12},{12,8},{16,20},{20,16},{24,28},{28,24},{1,5},{5... | collective-permute-start | bytes 2064392 | tf_op jit(solution)/shard_map/ppermute | solution.py:28
  68.2 29.1 %collective-permute-start.12 = (bf16[4,224,384]{2,1,0:T(8,128)(2,1)S(1)}, bf16[4,224,384]{2,1,0:T(8,128)(2,1)S(1)}, u32[]{:S(2)}, u32[]{:S(2)}) collective-permute-start(bf16[4,224,384]{2,1,0:T(8,128)(2,1)S(1)} %fusion.59), channel_id=1, source_target_pairs={{0,4},{4,0},{8,12},{12,8},{16,20},{20,16},{24,28},{28,24},{1,5},{5... | collective-permute-start | bytes 2064392 | tf_op jit(solution)/shard_map/ppermute | solution.py:28
  70.9 13.5 %collective-permute-start.17 = (bf16[4,224,256]{2,1,0:T(8,128)(2,1)S(1)}, bf16[4,224,256]{2,1,0:T(8,128)(2,1)S(1)}, u32[]{:S(2)}, u32[]{:S(2)}) collective-permute-start(bf16[4,224,256]{2,1,0:T(8,128)(2,1)S(1)} %bitcast.172), channel_id=1, source_target_pairs={{0,8},{4,12},{8,0},{12,4},{16,24},{20,28},{24,16},{28,20},{1,9},{5... | collective-permute-start | bytes 1376264 | tf_op jit(solution)/shard_map/ppermute | solution.py:28
  73.0 25.0 %collective-permute-start.16 = (bf16[4,224,256]{2,1,0:T(8,128)(2,1)S(1)}, bf16[4,224,256]{2,1,0:T(8,128)(2,1)S(1)}, u32[]{:S(2)}, u32[]{:S(2)}) collective-permute-start(bf16[4,224,256]{2,1,0:T(8,128)(2,1)S(1)} %bitcast.171), channel_id=1, source_target_pairs={{0,8},{4,12},{8,0},{12,4},{16,24},{20,28},{24,16},{28,20},{1,9},{5... | collective-permute-start | bytes 1376264 | tf_op jit(solution)/shard_map/ppermute | solution.py:28
  84.5 18.0 %collective-permute-start.18 = (bf16[4,224,256]{2,1,0:T(8,128)(2,1)S(1)}, bf16[4,224,256]{2,1,0:T(8,128)(2,1)S(1)}, u32[]{:S(2)}, u32[]{:S(2)}) collective-permute-start(bf16[4,224,256]{2,1,0:T(8,128)(2,1)S(1)} %fusion.55), channel_id=1, source_target_pairs={{0,2},{1,3},{2,0},{3,1},{4,6},{5,7},{6,4},{7,5},{8,10},{9,11},{10,... | collective-permute-start | bytes 1376264 | tf_op jit(solution)/shard_map/ppermute | solution.py:28
  85.2 40.1 %collective-permute-start.11 = (bf16[2,224,384]{2,1,0:T(8,128)(2,1)S(1)}, bf16[2,224,384]{2,1,0:T(8,128)(2,1)S(1)}, u32[]{:S(2)}, u32[]{:S(2)}) collective-permute-start(bf16[2,224,384]{2,1,0:T(8,128)(2,1)S(1)} %fusion.63), channel_id=1, source_target_pairs={{0,8},{4,12},{8,0},{12,4},{16,24},{20,28},{24,16},{28,20},{1,9},{5... | collective-permute-start | bytes 1032200 | tf_op jit(solution)/shard_map/ppermute | solution.py:28
  97.5 14.2 %collective-permute-start.13 = (bf16[2,224,384]{2,1,0:T(8,128)(2,1)S(1)}, bf16[2,224,384]{2,1,0:T(8,128)(2,1)S(1)}, u32[]{:S(2)}, u32[]{:S(2)}) collective-permute-start(bf16[2,224,384]{2,1,0:T(8,128)(2,1)S(1)} %fusion.64), channel_id=1, source_target_pairs={{0,8},{4,12},{8,0},{12,4},{16,24},{20,28},{24,16},{28,20},{1,9},{5... | collective-permute-start | bytes 1032200 | tf_op jit(solution)/shard_map/ppermute | solution.py:28
  102.7 8.5 %collective-permute-start.19 = (bf16[2,224,256]{2,1,0:T(8,128)(2,1)S(1)}, bf16[2,224,256]{2,1,0:T(8,128)(2,1)S(1)}, u32[]{:S(2)}, u32[]{:S(2)}) collective-permute-start(bf16[2,224,256]{2,1,0:T(8,128)(2,1)S(1)} %fusion.73), channel_id=1, source_target_pairs={{0,4},{4,0},{8,12},{12,8},{16,20},{20,16},{24,28},{28,24},{1,5},{5... | collective-permute-start | bytes 688136 | tf_op jit(solution)/shard_map/ppermute | solution.py:28
  104.0 20.7 %collective-permute-start.7 = (bf16[4,224,384]{2,1,0:T(8,128)(2,1)S(1)}, bf16[4,224,384]{2,1,0:T(8,128)(2,1)S(1)}, u32[]{:S(2)}, u32[]{:S(2)}) collective-permute-start(bf16[4,224,384]{2,1,0:T(8,128)(2,1)S(1)} %fusion.57), channel_id=1, source_target_pairs={{0,4},{4,0},{8,12},{12,8},{16,20},{20,16},{24,28},{28,24},{1,5},{5... | collective-permute-start | bytes 2064392 | tf_op jit(solution)/shard_map/ppermute | solution.py:28
  111.3 6.9 %collective-permute-start.20 = (bf16[1,224,256]{2,1,0:T(8,128)(2,1)S(1)}, bf16[1,224,256]{2,1,0:T(8,128)(2,1)S(1)}, u32[]{:S(2)}, u32[]{:S(2)}) collective-permute-start(bf16[1,224,256]{2,1,0:T(8,128)(2,1)S(1)} %dynamic-slice_convert_fusion.6), channel_id=1, source_target_pairs={{0,16},{4,20},{8,24},{12,28},{16,0},{20,4},{24,8},{28,12},{1,17},{... | collective-permute-start | bytes 344072 | tf_op jit(solution)/shard_map/ppermute | solution.py:28
  111.8 13.5 %collective-permute-start.14 = (bf16[2,224,384]{2,1,0:T(8,128)(2,1)S(1)}, bf16[2,224,384]{2,1,0:T(8,128)(2,1)S(1)}, u32[]{:S(2)}, u32[]{:S(2)}) collective-permute-start(bf16[2,224,384]{2,1,0:T(8,128)(2,1)S(1)} %fusion.60), channel_id=1, source_target_pairs={{0,2},{1,3},{2,0},{3,1},{4,6},{5,7},{6,4},{7,5},{8,10},{9,11},{10,... | collective-permute-start | bytes 1032200 | tf_op jit(solution)/shard_map/ppermute | solution.py:28
  124.8 12.5 %collective-permute-start.8 = (bf16[2,224,384]{2,1,0:T(8,128)(2,1)S(1)}, bf16[2,224,384]{2,1,0:T(8,128)(2,1)S(1)}, u32[]{:S(2)}, u32[]{:S(2)}) collective-permute-start(bf16[2,224,384]{2,1,0:T(8,128)(2,1)S(1)} %fusion.62), channel_id=1, source_target_pairs={{0,8},{4,12},{8,0},{12,4},{16,24},{20,28},{24,16},{28,20},{1,9},{5... | collective-permute-start | bytes 1032200 | tf_op jit(solution)/shard_map/ppermute | solution.py:28
  125.5 12.0 %collective-permute-start.15 = (bf16[1,224,384]{2,1,0:T(8,128)(2,1)S(1)}, bf16[1,224,384]{2,1,0:T(8,128)(2,1)S(1)}, u32[]{:S(2)}, u32[]{:S(2)}) collective-permute-start(bf16[1,224,384]{2,1,0:T(8,128)(2,1)S(1)} %dynamic-slice_convert_fusion.4), channel_id=1, source_target_pairs={{0,16},{4,20},{8,24},{12,28},{16,0},{20,4},{24,8},{28,12},{1,17},{... | collective-permute-start | bytes 516104 | tf_op jit(solution)/shard_map/ppermute | solution.py:28
  137.4 8.6 %collective-permute-start.9 = (bf16[1,224,384]{2,1,0:T(8,128)(2,1)S(1)}, bf16[1,224,384]{2,1,0:T(8,128)(2,1)S(1)}, u32[]{:S(2)}, u32[]{:S(2)}) collective-permute-start(bf16[1,224,384]{2,1,0:T(8,128)(2,1)S(1)} %dynamic-slice_convert_fusion.5), channel_id=1, source_target_pairs={{0,16},{4,20},{8,24},{12,28},{16,0},{20,4},{24,8},{28,12},{1,17},{... | collective-permute-start | bytes 516104 | tf_op jit(solution)/shard_map/ppermute | solution.py:28

commit v2 on v1

--- a/solution.py
+++ b/solution.py
@@ -117,25 +117,23 @@
         blocks = {step: block_value(c, step) for step in reversed(range(outer))}
         state.append((blocks, list(range(ctx_bits - 1, -1, -1))))
     for stage in range(len(orders[0])):
+        kept_parts, arrived = [], []
         for c in range(len(SHARES)):
             blocks, kept = state[c]
             axis, bit = orders[c][stage]
             if axis == "dp":
                 far = 1 << (bit - 1)
-                blocks = {
-                    step: blocks[step]
-                    + swap(blocks[step ^ far].astype(jnp.bfloat16), axis, bit).astype(jnp.float32)
-                    for step in blocks
-                    if not step & far
-                }
+                pairs = {step: (blocks[step], blocks[step ^ far]) for step in blocks if not step & far}
             else:
                 pairs = {step: split(blocks[step], bit, kept) for step in blocks}
-                blocks = {
-                    step: keep + swap(send.astype(jnp.bfloat16), axis, bit).astype(jnp.float32)
-                    for step, (keep, send) in pairs.items()
-                }
                 kept = [other for other in kept if other != bit]
-            state[c] = (blocks, kept)
+            kept_parts.append(({step: keep for step, (keep, _) in pairs.items()}, kept))
+            arrived.append({step: swap(send.astype(jnp.bfloat16), axis, bit) for step, (_, send) in pairs.items()})
+        arrived = lax.optimization_barrier(arrived)
+        state = [
+            ({step: keeps[step] + got[step].astype(jnp.float32) for step in keeps}, kept)
+            for (keeps, kept), got in zip(kept_parts, arrived)
+        ]
     weight_grad = jnp.concatenate(
         [blocks[0].reshape(ff_rows, -1) for blocks, _ in state], axis=1
     ) / jnp.sqrt(jnp.float32(seq_total))

time: 148 us -> 161 us (1.088)
  local copies, waits for them, and re-layouts: 16.4 us -> 33.8 us
  waiting for transfers between devices: 61.6 us -> 48.2 us
  other arithmetic: 23.9 us -> 29.8 us
  starting transfers between devices: 20.5 us -> 24.1 us
    ppermute x21, waiting for transfers between devices: 61.6 us -> 48.2 us  [swap(): return lax.ppermute(value, axis, [(i, i ^ 1 << bit) for i in range(size)])]
    slice x8, local copies, waits for them, and re-layouts: 0.09 us -> 9.34 us  [block_value(): term = term * hs[:, None] * scales[step][None, cols]]
    ppermute x21, starting transfers between devices: 20.5 us -> 24.1 us  [swap(): return lax.ppermute(value, axis, [(i, i ^ 1 << bit) for i in range(size)])]
    add x8, other arithmetic: 1.01 us -> 4.24 us  [on_device(): keeps[step] + got[step].astype(jnp.float32)]
    unnamed x11 -> x61, local copies, waits for them, and re-layouts: 2.82 us -> 5.26 us
    convert_element_type x12, local copies, waits for them, and re-layouts: 0.63 us -> 2.69 us  [on_device(): send.astype(jnp.bfloat16)]
    reshape x3, other arithmetic: 0.09 us -> 1.91 us  [on_device(): blocks[0].reshape(ff_rows, -1)]
  transfers between devices with their start and end apart: 21 -> 21, of which waited for: 8 -> 10; matrix products, arithmetic and copies ran while one was open for 30% -> 40% of each run, Pallas kernels for 0% -> 0%
where the time goes in v2:
time: 161 us
  waiting for transfers between devices  48.2 us (30%)
  local copies, waits for them, and re-layouts  33.8 us (21%)
  other arithmetic  29.8 us (19%)
  starting transfers between devices  24.1 us (15%)
  matrix products  23.7 us (15%)
    ppermute x21, waiting for transfers between devices, swap(): return lax.ppermute(value, axis, [(i, i ^ 1 << bit) for i in range(size)])  48.2 us
    ppermute x21, starting transfers between devices, swap(): return lax.ppermute(value, axis, [(i, i ^ 1 << bit) for i in range(size)])  24.1 us
    convert_element_type x4, other arithmetic, to_grid(): return jnp.where(scaled < 0, -snapped, snapped).astype(jnp.bfloat16)  16.5 us
    dot_general x12, matrix products, block_value(): lax.dot_general(hq, near[step][:, cols], (((0,), (0,)), ((), ())), prefer...  13.3 us
    dot_general x1, matrix products, on_device(): lax.dot_general(gdata, down_weight, (((1,), (1,)), ((), ())), preferred_e...  10.4 us
    dynamic_slice x6, local copies, waits for them, and re-layouts, on_device(): lax.dynamic_index_in_dim(gq, step ^ dp_pos // 2, 1, keepdims=False)  9.76 us
    slice x8, local copies, waits for them, and re-layouts, block_value(): term = term * hs[:, None] * scales[step][None, cols]  9.34 us
    unnamed x61, local copies, waits for them, and re-layouts  5.26 us
  transfers between devices with their start and end apart: 21, of which 10 were waited for; matrix products, arithmetic and copies ran while one was open for 40% of the time, Pallas kernels for 0%

profile of v2, /device:TPU:0, one launch (start us, length us, event | category | flops | bytes accessed | tf_op | source)
XLA Modules:
  0.0 160.6 jit_solution(5048890846732872720)
XLA Ops:
  0.6 2.4 %fusion.14 = bf16[4096]{0:T(1024)(128)(2,1)S(1)} fusion(bf16[1,384,4096]{2,1,0:T(8,128)(2,1)} %param.3), kind=kLoop, calls=%fused_computation.52 | loop fusion | flops 3141632 | bytes 3153920 | tf_op jit(solution)/shard_map/reduce_max | solution.py:23
  3.0 1.5 abs_reduce_fusion
  4.5 3.1 %collective-permute-start = (bf16[5888]{0:T(1024)(128)(2,1)S(1)}, bf16[5888]{0:T(1024)(128)(2,1)S(1)}, u32[]{:S(2)}, u32[]{:S(2)}) collective-permute-start(bf16[5888]{0:T(1024)(128)(2,1)S(1)} %pad_maximum_fusion), channel_id=1, source_target_pairs={{0,4},{4,0},{8,12},{12,8},{16,20},{20,16},{24,28},{28,24},{1,5},{5... | collective-permute-start | bytes 35336 | tf_op jit(solution)/shard_map/ppermute | solution.py:28
  7.6 1.7 %collective-permute-done = bf16[5888]{0:T(1024)(128)(2,1)S(1)} collective-permute-done((bf16[5888]{0:T(1024)(128)(2,1)S(1)}, bf16[5888]{0:T(1024)(128)(2,1)S(1)}, u32[]{:S(2)}, u32[]{:S(2)}) %collective-permute-start) | collective-permute-done | bytes 11808 | tf_op jit(solution)/shard_map/ppermute | solution.py:28
  9.3 2.1 %collective-permute-start.1 = (bf16[5888]{0:T(1024)(128)(2,1)S(1)}, bf16[5888]{0:T(1024)(128)(2,1)S(1)}, u32[]{:S(2)}, u32[]{:S(2)}) collective-permute-start(bf16[5888]{0:T(1024)(128)(2,1)S(1)} %fusion.82), channel_id=1, source_target_pairs={{0,8},{4,12},{8,0},{12,4},{16,24},{20,28},{24,16},{28,20},{1,9},{5... | collective-permute-start | bytes 35336 | tf_op jit(solution)/shard_map/ppermute | solution.py:28
  11.4 2.8 %copy.12 = bf16[1,384,4096]{1,2,0:T(8,128)(2,1)} copy(bf16[1,384,4096]{2,1,0:T(8,128)(2,1)S(1)} %copy-done) | data formatting | bytes 6291456 | tf_op args[0]
  14.3 2.7 %collective-permute-start.2 = (bf16[5888]{0:T(1024)(128)(2,1)S(1)}, bf16[5888]{0:T(1024)(128)(2,1)S(1)}, u32[]{:S(2)}, u32[]{:S(2)}) collective-permute-start(bf16[5888]{0:T(1024)(128)(2,1)S(1)} %max.16), channel_id=1, source_target_pairs={{0,16},{4,20},{8,24},{12,28},{16,0},{20,4},{24,8},{28,12},{1,17},{... | collective-permute-start | bytes 35336 | tf_op jit(solution)/shard_map/ppermute | solution.py:28
  16.9 2.7 %dynamic-slice_bitcast_fusion = bf16[384,2,1024]{0,2,1:T(8,128)(2,1)} fusion(bf16[384,2,2,1024]{0,3,2,1:T(8,128)(2,1)} %bitcast.137, s32[]{:T(128)S(6)} %select_n.278), kind=kLoop, calls=%fused_computation.105 | loop fusion | bytes 3145732 | tf_op jit(solution)/shard_map/jit(dynamic_index_in_dim)/squeeze | solution.py:53
  20.9 2.7 %fusion.51 = bf16[384,1792]{1,0:T(8,128)(2,1)S(1)} fusion(f32[1792]{0:T(1024)S(1)} %get-tuple-element.61, bf16[1,384,1792]{2,1,0:T(8,128)(2,1)S(1)} %copy-done.2), kind=kLoop, calls=%fused_computation.103 | loop fusion | flops 21331968 | bytes 2759680 | tf_op jit(solution)/shard_map/convert_element_type | solution.py:19
  23.7 1.7 %collective-permute-done.4 = bf16[5888]{0:T(1024)(128)(2,1)S(1)} collective-permute-done((bf16[5888]{0:T(1024)(128)(2,1)S(1)}, bf16[5888]{0:T(1024)(128)(2,1)S(1)}, u32[]{:S(2)}, u32[]{:S(2)}) %collective-permute-start.4) | collective-permute-done | bytes 11808 | tf_op jit(solution)/shard_map/ppermute | solution.py:28
  25.5 4.4 %fusion.17 = bf16[384,2,1024]{0,2,1:T(8,128)(2,1)S(1)} fusion(f32[2,1024]{1,0:T(2,128)S(1)} %bitcast.175, bf16[384,2,2,1024]{0,3,2,1:T(8,128)(2,1)} %bitcast.138, s32[]{:T(128)S(6)} %select_n.256), kind=kLoop, calls=%fused_computation.56 | loop fusion | flops 24379392 | bytes 3153924 | tf_op jit(solution)/shard_map/convert_element_type | solution.py:19
  30.5 1.4 constant_dynamic-slice_fusion.9
  33.1 1.4 copy.13
  34.5 2.3 %copy.14 = bf16[384,1,1024]{2,0,1:T(8,128)(2,1)} copy(bf16[384,1,1024]{0,2,1:T(8,128)(2,1)} %get-tuple-element.56) | data formatting | bytes 1572864 | tf_op jit(solution)/shard_map/jit(dynamic_index_in_dim)/dynamic_slice | solution.py:78
  36.8 1.2 slice.140
  38.0 1.2 slice.139
  39.3 1.2 slice.138
  40.5 1.3 slice_reduce_fusion
  41.7 1.3 slice_reduce_fusion.1
  43.0 1.3 slice_reduce_fusion.2
  44.3 1.3 slice_reduce_fusion.3
  45.6 1.3 slice_multiply_fusion
  46.9 4.7 %fusion.49 = bf16[384,1792]{1,0:T(8,128)(2,1)} fusion(bf16[384,1792]{1,0:T(8,128)(2,1)} %collective-permute-done.3, f32[1792]{0:T(1024)S(1)} %get-tuple-element.64), kind=kLoop, calls=%fused_computation.100 | loop fusion | flops 21331968 | bytes 2759680 | tf_op jit(solution)/shard_map/convert_element_type | solution.py:19
  51.5 4.6 %fusion.16 = bf16[384,2,1024]{0,2,1:T(8,128)(2,1)S(1)} fusion(bf16[384,2,1024]{0,2,1:T(8,128)(2,1)} %collective-permute-done.5, f32[2,1024]{1,0:T(2,128)S(1)} %bitcast.174), kind=kLoop, calls=%fused_computation.55 | loop fusion | flops 24379392 | bytes 3153920 | tf_op jit(solution)/shard_map/convert_element_type | solution.py:19
  56.2 1.0 constant_dynamic-slice_fusion.5
  57.2 1.2 copy.18
  58.5 2.4 %copy.17 = bf16[384,1,1024]{2,0,1:T(8,128)(2,1)} copy(bf16[384,1,1024]{0,2,1:T(8,128)(2,1)} %get-tuple-element.59) | data formatting | bytes 1572864 | tf_op jit(solution)/shard_map/jit(dynamic_index_in_dim)/dynamic_slice | solution.py:78
  60.9 2.0 %fusion.34 = f32[1792,256]{1,0:T(8,128)S(1)} fusion(bf16[384,1792]{1,0:T(8,128)(2,1)} %fusion.49, f32[256]{0:T(256)S(1)} %bitcast.180, f32[1792]{0:T(1024)S(1)} %copy-done.20, bf16[384,1024]{1,0:T(8,128)(2,1)} %bitcast.169), kind=kOutput, calls=%fused_computation.80 | convolution fusion | flops 353239040 | bytes 3416064 | tf_op jit(solution)/shard_map/dot_general | solution.py:98
  63.8 0.9 collective-permute-start.10
  66.2 1.3 collective-permute-start.9
  67.5 1.1 fusion.29
  68.6 1.1 fusion.28
  69.8 1.6 collective-permute-start.8
  71.4 1.1 fusion.26
  72.5 1.1 fusion.23
  73.6 1.2 fusion.33
  74.8 1.6 collective-permute-start.6
  76.4 1.1 fusion.25
  78.1 1.1 fusion.20
  79.3 1.3 fusion.19
  80.7 5.6 %collective-permute-done.9 = bf16[4,224,256]{2,1,0:T(8,128)(2,1)S(1)} collective-permute-done((bf16[4,224,256]{2,1,0:T(8,128)(2,1)S(1)}, bf16[4,224,256]{2,1,0:T(8,128)(2,1)S(1)}, u32[]{:S(2)}, u32[]{:S(2)}) %collective-permute-start.9) | collective-permute-done | bytes 458784 | tf_op jit(solution)/shard_map/ppermute | solution.py:28
  86.2 2.0 %collective-permute-done.8 = bf16[4,224,384]{2,1,0:T(8,128)(2,1)S(1)} collective-permute-done((bf16[4,224,384]{2,1,0:T(8,128)(2,1)S(1)}, bf16[4,224,384]{2,1,0:T(8,128)(2,1)S(1)}, u32[]{:S(2)}, u32[]{:S(2)}) %collective-permute-start.8) | collective-permute-done | bytes 688160 | tf_op jit(solution)/shard_map/ppermute | solution.py:28
  88.2 13.4 %collective-permute-done.7 = bf16[4,224,384]{2,1,0:T(8,128)(2,1)S(1)} collective-permute-done((bf16[4,224,384]{2,1,0:T(8,128)(2,1)S(1)}, bf16[4,224,384]{2,1,0:T(8,128)(2,1)S(1)}, u32[]{:S(2)}, u32[]{:S(2)}) %collective-permute-start.7) | collective-permute-done | bytes 688160 | tf_op jit(solution)/shard_map/ppermute | solution.py:28
  101.5 4.7 %collective-permute-done.6 = bf16[8,224,384]{2,1,0:T(8,128)(2,1)S(1)} collective-permute-done((bf16[8,224,384]{2,1,0:T(8,128)(2,1)S(1)}, bf16[8,224,384]{2,1,0:T(8,128)(2,1)S(1)}, u32[]{:S(2)}, u32[]{:S(2)}) %collective-permute-start.6) | collective-permute-done | bytes 1376288 | tf_op jit(solution)/shard_map/ppermute | solution.py:28
  106.4 1.5 collective-permute-start.14
  108.1 1.0 collective-permute-start.13
  110.2 1.2 collective-permute-start.12
  111.4 7.7 %collective-permute-done.13 = bf16[2,224,384]{2,1,0:T(8,128)(2,1)S(1)} collective-permute-done((bf16[2,224,384]{2,1,0:T(8,128)(2,1)S(1)}, bf16[2,224,384]{2,1,0:T(8,128)(2,1)S(1)}, u32[]{:S(2)}, u32[]{:S(2)}) %collective-permute-start.13) | collective-permute-done | bytes 344096 | tf_op jit(solution)/shard_map/ppermute | solution.py:28
  119.1 4.6 %collective-permute-done.12 = bf16[2,224,384]{2,1,0:T(8,128)(2,1)S(1)} collective-permute-done((bf16[2,224,384]{2,1,0:T(8,128)(2,1)S(1)}, bf16[2,224,384]{2,1,0:T(8,128)(2,1)S(1)}, u32[]{:S(2)}, u32[]{:S(2)}) %collective-permute-start.12) | collective-permute-done | bytes 344096 | tf_op jit(solution)/shard_map/ppermute | solution.py:28
  123.7 1.1 collective-permute-done.11
  125.6 0.8 fusion.64
  126.4 1.0 collective-permute-start.15
  127.6 0.9 copy-done.4
  129.7 5.8 %collective-permute-done.17 = bf16[2,224,256]{2,1,0:T(8,128)(2,1)} collective-permute-done((bf16[2,224,256]{2,1,0:T(8,128)(2,1)}, bf16[2,224,256]{2,1,0:T(8,128)(2,1)}, u32[]{:S(2)}, u32[]{:S(2)}) %collective-permute-start.17) | collective-permute-done | bytes 229408 | tf_op jit(solution)/shard_map/ppermute | solution.py:28
  135.5 1.3 bitcast_add_fusion.8
  138.0 1.2 fusion.60
  139.8 2.6 %collective-permute-start.19 = (bf16[1,224,384]{2,1,0:T(8,128)(2,1)}, bf16[1,224,384]{2,1,0:T(8,128)(2,1)S(1)}, u32[]{:S(2)}, u32[]{:S(2)}) collective-permute-start(bf16[1,224,384]{2,1,0:T(8,128)(2,1)} %dynamic-slice_convert_fusion.4), channel_id=1, source_target_pairs={{0,16},{4,20},{8,24},{12,28},{16,0},{20,4},{24,8},{28,12},{1,17},{... | collective-permute-start | bytes 516104 | tf_op jit(solution)/shard_map/ppermute | solution.py:28
  142.4 1.0 bitcast_add_fusion.7
  143.9 10.4 %fusion.52 = bf16[1,384,1792]{2,1,0:T(8,128)(2,1)} fusion(bf16[1792,4096]{1,0:T(8,128)(2,1)} %param.5, bf16[1,384,4096]{2,1,0:T(8,128)(2,1)S(1)} %copy-done.1), kind=kOutput, calls=%fused_computation.104 | convolution fusion | flops 5637832704 | bytes 19202048 | tf_op jit(solution)/shard_map/dot_general | solution.py:67
  154.3 1.3 dynamic_slice.173
  155.7 1.3 dynamic_slice.172
  157.7 1.0 add_bitcast_fusion
  158.7 0.9 add_bitcast_fusion.2
  159.6 1.0 maximum_multiply_fusion
  (117 shorter events, 12.8 us)
Async XLA Ops:
  0.6 10.8 %copy-start = (bf16[1,384,4096]{2,1,0:T(8,128)(2,1)S(1)}, bf16[1,384,4096]{2,1,0:T(8,128)(2,1)}, u32[]{:S(2)}) copy-start(bf16[1,384,4096]{2,1,0:T(8,128)(2,1)} %param.3) | copy-start | bytes 9437188
  4.5 4.7 %collective-permute-start = (bf16[5888]{0:T(1024)(128)(2,1)S(1)}, bf16[5888]{0:T(1024)(128)(2,1)S(1)}, u32[]{:S(2)}, u32[]{:S(2)}) collective-permute-start(bf16[5888]{0:T(1024)(128)(2,1)S(1)} %pad_maximum_fusion), channel_id=1, source_target_pairs={{0,4},{4,0},{8,12},{12,8},{16,20},{20,16},{24,28},{28,24},{1,5},{5... | collective-permute-start | bytes 35336 | tf_op jit(solution)/shard_map/ppermute | solution.py:28
  9.3 5.0 %collective-permute-start.1 = (bf16[5888]{0:T(1024)(128)(2,1)S(1)}, bf16[5888]{0:T(1024)(128)(2,1)S(1)}, u32[]{:S(2)}, u32[]{:S(2)}) collective-permute-start(bf16[5888]{0:T(1024)(128)(2,1)S(1)} %fusion.82), channel_id=1, source_target_pairs={{0,8},{4,12},{8,0},{12,4},{16,24},{20,28},{24,16},{28,20},{1,9},{5... | collective-permute-start | bytes 35336 | tf_op jit(solution)/shard_map/ppermute | solution.py:28
  14.3 5.4 %copy-start.2 = (bf16[1,384,1792]{2,1,0:T(8,128)(2,1)S(1)}, bf16[1,384,1792]{2,1,0:T(8,128)(2,1)}, u32[]{:S(2)}) copy-start(bf16[1,384,1792]{2,1,0:T(8,128)(2,1)} %param.4) | copy-start | bytes 4128772
  14.3 5.9 %collective-permute-start.2 = (bf16[5888]{0:T(1024)(128)(2,1)S(1)}, bf16[5888]{0:T(1024)(128)(2,1)S(1)}, u32[]{:S(2)}, u32[]{:S(2)}) collective-permute-start(bf16[5888]{0:T(1024)(128)(2,1)S(1)} %max.16), channel_id=1, source_target_pairs={{0,16},{4,20},{8,24},{12,28},{16,0},{20,4},{24,8},{28,12},{1,17},{... | collective-permute-start | bytes 35336 | tf_op jit(solution)/shard_map/ppermute | solution.py:28
  19.7 31.9 %collective-permute-start.5 = (bf16[384,2,1024]{0,2,1:T(8,128)(2,1)}, bf16[384,2,1024]{0,2,1:T(8,128)(2,1)}, u32[]{:S(2)}, u32[]{:S(2)}) collective-permute-start(bf16[384,2,1024]{0,2,1:T(8,128)(2,1)} %dynamic-slice_bitcast_fusion), channel_id=1, source_target_pairs={{0,1},{1,0},{2,3},{3,2},{4,5},{5,4},{6,7},{7,6},{8,9},{9,8},{10,11... | collective-permute-start | bytes 4718600 | tf_op jit(solution)/shard_map/ppermute | solution.py:28
  19.7 27.2 %collective-permute-start.3 = (bf16[384,1792]{1,0:T(8,128)(2,1)S(1)}, bf16[384,1792]{1,0:T(8,128)(2,1)}, u32[]{:S(2)}, u32[]{:S(2)}) collective-permute-start(bf16[384,1792]{1,0:T(8,128)(2,1)S(1)} %bitcast.150), channel_id=1, source_target_pairs={{0,1},{1,0},{2,3},{3,2},{4,5},{5,4},{6,7},{7,6},{8,9},{9,8},{10,11... | collective-permute-start | bytes 4128776 | tf_op jit(solution)/shard_map/ppermute | solution.py:28
  20.2 5.2 %collective-permute-start.4 = (bf16[5888]{0:T(1024)(128)(2,1)S(1)}, bf16[5888]{0:T(1024)(128)(2,1)S(1)}, u32[]{:S(2)}, u32[]{:S(2)}) collective-permute-start(bf16[5888]{0:T(1024)(128)(2,1)S(1)} %get-tuple-element.55), channel_id=1, source_target_pairs={{0,1},{1,0},{2,3},{3,2},{4,5},{5,4},{6,7},{7,6},{8,9},{9,8},{10,11... | collective-permute-start | bytes 35336 | tf_op jit(solution)/shard_map/ppermute | solution.py:28
  23.6 8.3 %copy-start.14 = (f32[4096]{0:T(1024)}, f32[4096]{0:T(1024)S(1)}, u32[]{:S(2)}) copy-start(f32[4096]{0:T(1024)S(1)} %slice.127) | copy-start | bytes 49156
  25.4 6.5 %copy-start.13 = (f32[5888]{0:T(1024)}, f32[5888]{0:T(1024)S(1)}, u32[]{:S(2)}) copy-start(f32[5888]{0:T(1024)S(1)} %convert_maximum_fusion) | copy-start | bytes 70660
  30.5 2.6 %copy-start.15 = (f32[1,1024]{1,0:T(1,128)}, f32[1,1024]{1,0:T(1,128)S(1)}, u32[]{:S(2)}) copy-start(f32[1,1024]{1,0:T(1,128)S(1)} %get-tuple-element.71) | copy-start | bytes 12292
  56.2 4.7 %copy-start.20 = (f32[1792]{0:T(1024)S(1)}, f32[1792]{0:T(1024)}, u32[]{:S(2)}) copy-start(f32[1792]{0:T(1024)} %get-tuple-element.63) | copy-start | bytes 21508
  56.2 4.7 %copy-start.28 = (f32[1,256]{1,0:T(1,128)S(1)}, f32[1,256]{1,0:T(1,128)}, u32[]{:S(2)}) copy-start(f32[1,256]{1,0:T(1,128)} %slice.141) | copy-start | bytes 3076
  58.4 4.5 %copy-start.3 = (bf16[384,1,1024]{2,0,1:T(8,128)(2,1)S(1)}, bf16[384,1,1024]{2,0,1:T(8,128)(2,1)}, u32[]{:S(2)}) copy-start(bf16[384,1,1024]{2,0,1:T(8,128)(2,1)} %copy.14) | copy-start | bytes 2359300
  58.4 4.5 %copy-start.22 = (f32[1,256]{1,0:T(1,128)S(1)}, f32[1,256]{1,0:T(1,128)}, u32[]{:S(2)}) copy-start(f32[1,256]{1,0:T(1,128)} %slice.140) | copy-start | bytes 3076
  62.9 1.7 %copy-start.7 = (bf16[384,1792]{1,0:T(8,128)(2,1)S(1)}, bf16[384,1792]{1,0:T(8,128)(2,1)}, u32[]{:S(2)}) copy-start(bf16[384,1792]{1,0:T(8,128)(2,1)} %fusion.49) | copy-start | bytes 4128772
  62.9 1.7 %copy-start.8 = (bf16[384,1,1024]{2,0,1:T(8,128)(2,1)S(1)}, bf16[384,1,1024]{2,0,1:T(8,128)(2,1)}, u32[]{:S(2)}) copy-start(bf16[384,1,1024]{2,0,1:T(8,128)(2,1)} %copy.17) | copy-start | bytes 2359300
  62.9 1.7 %copy-start.27 = (f32[1,256]{1,0:T(1,128)S(1)}, f32[1,256]{1,0:T(1,128)}, u32[]{:S(2)}) copy-start(f32[1,256]{1,0:T(1,128)} %slice.139) | copy-start | bytes 3076
  63.7 1.6 %copy-start.21 = (f32[1,256]{1,0:T(1,128)S(1)}, f32[1,256]{1,0:T(1,128)}, u32[]{:S(2)}) copy-start(f32[1,256]{1,0:T(1,128)} %slice.138) | copy-start | bytes 3076
  63.8 16.9 %collective-permute-start.10 = (bf16[4,224,256]{2,1,0:T(8,128)(2,1)S(1)}, bf16[4,224,256]{2,1,0:T(8,128)(2,1)S(1)}, u32[]{:S(2)}, u32[]{:S(2)}) collective-permute-start(bf16[4,224,256]{2,1,0:T(8,128)(2,1)S(1)} %bitcast.172), channel_id=1, source_target_pairs={{0,8},{4,12},{8,0},{12,4},{16,24},{20,28},{24,16},{28,20},{1,9},{5... | collective-permute-start | bytes 1376264 | tf_op jit(solution)/shard_map/ppermute | solution.py:28
  65.4 2.1 %copy-start.9 = (bf16[384,1,1024]{2,0,1:T(8,128)(2,1)S(1)}, bf16[384,1,1024]{2,0,1:T(8,128)(2,1)}, u32[]{:S(2)}) copy-start(bf16[384,1,1024]{2,0,1:T(8,128)(2,1)} %copy.18) | copy-start | bytes 2359300
  65.4 2.1 %copy-start.26 = (f32[384]{0:T(512)S(1)}, f32[384]{0:T(512)}, u32[]{:S(2)}) copy-start(f32[384]{0:T(512)} %get-tuple-element.48) | copy-start | bytes 4612
  66.2 20.0 %collective-permute-start.9 = (bf16[4,224,256]{2,1,0:T(8,128)(2,1)S(1)}, bf16[4,224,256]{2,1,0:T(8,128)(2,1)S(1)}, u32[]{:S(2)}, u32[]{:S(2)}) collective-permute-start(bf16[4,224,256]{2,1,0:T(8,128)(2,1)S(1)} %bitcast.173), channel_id=1, source_target_pairs={{0,8},{4,12},{8,0},{12,4},{16,24},{20,28},{24,16},{28,20},{1,9},{5... | collective-permute-start | bytes 1376264 | tf_op jit(solution)/shard_map/ppermute | solution.py:28
  67.5 1.1 copy-start.19
  68.6 2.8 %copy-start.25 = (f32[384]{0:T(512)S(1)}, f32[384]{0:T(512)}, u32[]{:S(2)}) copy-start(f32[384]{0:T(512)} %get-tuple-element.52) | copy-start | bytes 4612
  69.8 18.4 %collective-permute-start.8 = (bf16[4,224,384]{2,1,0:T(8,128)(2,1)S(1)}, bf16[4,224,384]{2,1,0:T(8,128)(2,1)S(1)}, u32[]{:S(2)}, u32[]{:S(2)}) collective-permute-start(bf16[4,224,384]{2,1,0:T(8,128)(2,1)S(1)} %fusion.59), channel_id=1, source_target_pairs={{0,4},{4,0},{8,12},{12,8},{16,20},{20,16},{24,28},{28,24},{1,5},{5... | collective-permute-start | bytes 2064392 | tf_op jit(solution)/shard_map/ppermute | solution.py:28
  71.4 1.1 copy-start.24
  72.5 1.1 copy-start.18
  73.6 2.8 %copy-start.17 = (f32[384]{0:T(512)S(1)}, f32[384]{0:T(512)}, u32[]{:S(2)}) copy-start(f32[384]{0:T(512)} %get-tuple-element.50) | copy-start | bytes 4612
  74.8 31.4 %collective-permute-start.6 = (bf16[8,224,384]{2,1,0:T(8,128)(2,1)S(1)}, bf16[8,224,384]{2,1,0:T(8,128)(2,1)S(1)}, u32[]{:S(2)}, u32[]{:S(2)}) collective-permute-start(bf16[8,224,384]{2,1,0:T(8,128)(2,1)S(1)} %bitcast.165), channel_id=1, source_target_pairs={{0,2},{1,3},{2,0},{3,1},{4,6},{5,7},{6,4},{7,5},{8,10},{9,11},{10,... | collective-permute-start | bytes 4128776 | tf_op jit(solution)/shard_map/ppermute | solution.py:28
  76.4 1.8 %copy-start.23 = (f32[384]{0:T(512)S(1)}, f32[384]{0:T(512)}, u32[]{:S(2)}) copy-start(f32[384]{0:T(512)} %get-tuple-element.53) | copy-start | bytes 4612
  77.6 24.0 %collective-permute-start.7 = (bf16[4,224,384]{2,1,0:T(8,128)(2,1)S(1)}, bf16[4,224,384]{2,1,0:T(8,128)(2,1)S(1)}, u32[]{:S(2)}, u32[]{:S(2)}) collective-permute-start(bf16[4,224,384]{2,1,0:T(8,128)(2,1)S(1)} %fusion.58), channel_id=1, source_target_pairs={{0,4},{4,0},{8,12},{12,8},{16,20},{20,16},{24,28},{28,24},{1,5},{5... | collective-permute-start | bytes 2064392 | tf_op jit(solution)/shard_map/ppermute | solution.py:28
  78.1 1.2 copy-start.16
  106.4 17.3 %collective-permute-start.14 = (bf16[4,224,256]{2,1,0:T(8,128)(2,1)S(1)}, bf16[4,224,256]{2,1,0:T(8,128)(2,1)S(1)}, u32[]{:S(2)}, u32[]{:S(2)}) collective-permute-start(bf16[4,224,256]{2,1,0:T(8,128)(2,1)S(1)} %fusion.56), channel_id=1, source_target_pairs={{0,2},{1,3},{2,0},{3,1},{4,6},{5,7},{6,4},{7,5},{8,10},{9,11},{10,... | collective-permute-start | bytes 1376264 | tf_op jit(solution)/shard_map/ppermute | solution.py:28
  108.1 11.0 %collective-permute-start.13 = (bf16[2,224,384]{2,1,0:T(8,128)(2,1)S(1)}, bf16[2,224,384]{2,1,0:T(8,128)(2,1)S(1)}, u32[]{:S(2)}, u32[]{:S(2)}) collective-permute-start(bf16[2,224,384]{2,1,0:T(8,128)(2,1)S(1)} %fusion.63), channel_id=1, source_target_pairs={{0,8},{4,12},{8,0},{12,4},{16,24},{20,28},{24,16},{28,20},{1,9},{5... | collective-permute-start | bytes 1032200 | tf_op jit(solution)/shard_map/ppermute | solution.py:28
  109.4 15.4 %collective-permute-start.11 = (bf16[4,224,384]{2,1,0:T(8,128)(2,1)S(1)}, bf16[4,224,384]{2,1,0:T(8,128)(2,1)S(1)}, u32[]{:S(2)}, u32[]{:S(2)}) collective-permute-start(bf16[4,224,384]{2,1,0:T(8,128)(2,1)S(1)} %fusion.57), channel_id=1, source_target_pairs={{0,4},{4,0},{8,12},{12,8},{16,20},{20,16},{24,28},{28,24},{1,5},{5... | collective-permute-start | bytes 2064392 | tf_op jit(solution)/shard_map/ppermute | solution.py:28
  110.2 13.5 %collective-permute-start.12 = (bf16[2,224,384]{2,1,0:T(8,128)(2,1)S(1)}, bf16[2,224,384]{2,1,0:T(8,128)(2,1)S(1)}, u32[]{:S(2)}, u32[]{:S(2)}) collective-permute-start(bf16[2,224,384]{2,1,0:T(8,128)(2,1)S(1)} %fusion.62), channel_id=1, source_target_pairs={{0,8},{4,12},{8,0},{12,4},{16,24},{20,28},{24,16},{28,20},{1,9},{5... | collective-permute-start | bytes 1032200 | tf_op jit(solution)/shard_map/ppermute | solution.py:28
  123.7 2.7 %copy-start.11 = (bf16[2,224,384]{2,1,0:T(8,128)(2,1)}, bf16[2,224,384]{2,1,0:T(8,128)(2,1)S(1)}, u32[]{:S(2)}) copy-start(bf16[2,224,384]{2,1,0:T(8,128)(2,1)S(1)} %collective-permute-done.12) | copy-start | bytes 1032196
  124.9 10.6 %collective-permute-start.16 = (bf16[2,224,384]{2,1,0:T(8,128)(2,1)S(1)}, bf16[2,224,384]{2,1,0:T(8,128)(2,1)}, u32[]{:S(2)}, u32[]{:S(2)}) collective-permute-start(bf16[2,224,384]{2,1,0:T(8,128)(2,1)S(1)} %fusion.61), channel_id=1, source_target_pairs={{0,2},{1,3},{2,0},{3,1},{4,6},{5,7},{6,4},{7,5},{8,10},{9,11},{10,... | collective-permute-start | bytes 1032200 | tf_op jit(solution)/shard_map/ppermute | solution.py:28
  126.4 9.1 %collective-permute-start.15 = (bf16[2,224,384]{2,1,0:T(8,128)(2,1)}, bf16[2,224,384]{2,1,0:T(8,128)(2,1)S(1)}, u32[]{:S(2)}, u32[]{:S(2)}) collective-permute-start(bf16[2,224,384]{2,1,0:T(8,128)(2,1)} %fusion.64), channel_id=1, source_target_pairs={{0,8},{4,12},{8,0},{12,4},{16,24},{20,28},{24,16},{28,20},{1,9},{5... | collective-permute-start | bytes 1032200 | tf_op jit(solution)/shard_map/ppermute | solution.py:28
  127.6 0.9 copy-start.4
  129.2 6.3 %collective-permute-start.17 = (bf16[2,224,256]{2,1,0:T(8,128)(2,1)}, bf16[2,224,256]{2,1,0:T(8,128)(2,1)}, u32[]{:S(2)}, u32[]{:S(2)}) collective-permute-start(bf16[2,224,256]{2,1,0:T(8,128)(2,1)} %fusion.73), channel_id=1, source_target_pairs={{0,4},{4,0},{8,12},{12,8},{16,20},{20,16},{24,28},{28,24},{1,5},{5... | collective-permute-start | bytes 688136 | tf_op jit(solution)/shard_map/ppermute | solution.py:28
  129.7 14.2 %copy-start.1 = (bf16[1,384,4096]{2,1,0:T(8,128)(2,1)S(1)}, bf16[1,384,4096]{2,1,0:T(8,128)(2,1)}, u32[]{:S(2)}) copy-start(bf16[1,384,4096]{2,1,0:T(8,128)(2,1)} %param.3) | copy-start | bytes 9437188
  135.5 1.4 copy-start.10
  136.9 0.8 copy-start.5
  137.6 19.4 %collective-permute-start.20 = (bf16[1,224,256]{2,1,0:T(8,128)(2,1)S(1)}, bf16[1,224,256]{2,1,0:T(8,128)(2,1)}, u32[]{:S(2)}, u32[]{:S(2)}) collective-permute-start(bf16[1,224,256]{2,1,0:T(8,128)(2,1)S(1)} %dynamic-slice_convert_fusion.6), channel_id=1, source_target_pairs={{0,16},{4,20},{8,24},{12,28},{16,0},{20,4},{24,8},{28,12},{1,17},{... | collective-permute-start | bytes 344072 | tf_op jit(solution)/shard_map/ppermute | solution.py:28
  139.8 17.1 %collective-permute-start.19 = (bf16[1,224,384]{2,1,0:T(8,128)(2,1)}, bf16[1,224,384]{2,1,0:T(8,128)(2,1)S(1)}, u32[]{:S(2)}, u32[]{:S(2)}) collective-permute-start(bf16[1,224,384]{2,1,0:T(8,128)(2,1)} %dynamic-slice_convert_fusion.4), channel_id=1, source_target_pairs={{0,16},{4,20},{8,24},{12,28},{16,0},{20,4},{24,8},{28,12},{1,17},{... | collective-permute-start | bytes 516104 | tf_op jit(solution)/shard_map/ppermute | solution.py:28
  143.5 15.2 %copy-start.6 = (f32[2,224,256]{2,1,0:T(8,128)S(1)}, f32[2,224,256]{2,1,0:T(8,128)}, u32[]{:S(2)}) copy-start(f32[2,224,256]{2,1,0:T(8,128)} %copy-done.5) | copy-start | bytes 1376260
  143.5 14.1 %collective-permute-start.18 = (bf16[1,224,384]{2,1,0:T(8,128)(2,1)S(1)}, bf16[1,224,384]{2,1,0:T(8,128)(2,1)S(1)}, u32[]{:S(2)}, u32[]{:S(2)}) collective-permute-start(bf16[1,224,384]{2,1,0:T(8,128)(2,1)S(1)} %dynamic-slice_convert_fusion.5), channel_id=1, source_target_pairs={{0,16},{4,20},{8,24},{12,28},{16,0},{20,4},{24,8},{28,12},{1,17},{... | collective-permute-start | bytes 516104 | tf_op jit(solution)/shard_map/ppermute | solution.py:28
  157.0 0.7 copy-start.12
